TPU v7x, 32 devices: a whole 2x2x4 slice. The times are simulated.
32 devices in a mesh: shard: 16 (over z, x, core), task: 2 (over y).
Axes of the slice: x: 2, y: 2, z: 4, core: 2. Of those that a mesh axis runs over, the one named last changes fastest.
Arguments:
- task_deltas: bfloat16 [2, 4, 256, 16384], P('task', None, 'shard')
- rank_scores: int32 [2, 4, 256, 16384], P('task', None, 'shard'), may hold values from 0 to 1073741823
- keep_limits: int32 [2, 4, 8], P('task'), may hold values from 268435456 to 805306367
Outputs:
- merged: bfloat16 [4, 256, 16384], P(None, 'shard', 'task')
All inputs are finite; a program needn't handle non-finite values.
Results may differ from a plain program's by a relative error of at most 0.0051.
Values may be sent and summed in bfloat16 or wider, within the bound.
A program may use at most 64 MiB of HBM per device.

v0:
```python
import jax
import jax.numpy as jnp
from jax import lax
from jax.sharding import PartitionSpec as P

EXPERTS = 8
FF = 16384


def swapped(value, axis, stride):
    mask = 2**stride
    pairs = [(source, source ^ mask) for source in range(lax.axis_size(axis))]
    return lax.ppermute(value, axis, pairs)


def keep_probability(column_sums, grand_sum, row_total):
    column_mean = column_sums / row_total
    grand_mean = grand_sum / (EXPERTS * row_total * FF)
    return (0.2 + 0.7 * column_mean / (column_mean + grand_mean)).astype(jnp.bfloat16)


def on_device(task_deltas, rank_scores, keep_limits):
    groups = lax.axis_size("shard") // EXPERTS
    expert = lax.axis_index("shard") // groups
    row_count = task_deltas.shape[2]
    rows_whole = row_count * groups
    width_all = task_deltas.shape[3]
    selector = jnp.arange(EXPERTS, dtype=jnp.int32) == expert
    results = []
    for layer_at in range(task_deltas.shape[1]):
        change = task_deltas[0, layer_at].astype(jnp.float32)
        magnitude = jnp.sum(jnp.abs(change), axis=0)
        group_total = magnitude
        for bit_at in range(groups.bit_length() - 1):
            group_total = group_total + swapped(group_total, "shard", bit_at)
        grand_sum = lax.psum(jnp.sum(magnitude), "shard")
        rounded = lax.optimization_barrier(keep_probability(group_total, grand_sum, rows_whole))
        probability = rounded.astype(jnp.float32)
        own_limit = jnp.sum(jnp.where(selector, keep_limits[0, layer_at], 0))
        retained = jnp.where(
            rank_scores[0, layer_at] < own_limit, change / probability[None, :], jnp.float32(0.0)
        )
        summed = lax.psum(retained, "task")
        columns = width_all // lax.axis_size("task")
        portion = lax.dynamic_slice_in_dim(summed, lax.axis_index("task") * columns, columns, 1)
        results.append(portion.astype(jnp.bfloat16))
    return jnp.stack(results)


def solution(mesh):
    return jax.shard_map(
        on_device,
        mesh=mesh,
        in_specs=(
            P("task", None, "shard", None),
            P("task", None, "shard", None),
            P("task", None, None),
        ),
        out_specs=P(None, "shard", "task"),
        check_vma=False,
    )
```

profile of v0, /device:TPU:0, one launch (start us, length us, event | category | flops | bytes accessed | tf_op | source)
XLA Modules:
  0.0 146.4 jit_solution(15803664491565942427)
XLA Ops:
  0.0 0.0 copy-start
  0.0 0.0 copy-start.1
  0.0 3.3 %fusion = (f32[]{:T(128)}, f32[]{:T(128)}, f32[]{:T(128)}, f32[]{:T(128)}, f32[16384]{0:T(1024)S(1)}, /*index=5*/f32[16384]{0:T(1024)S(1)}, f32[16384]{0:T(1024)S(1)}, f32[16384]{0:T(1024)S(1)}) fusion(bf16[1,4,16,16384]{3,2,1,0:T(8,128)(2,1)} %param.3), kind=kLoop, calls=%fused_computation.8 | loop fusion | flops 4128764 | bytes 2359312 | tf_op jit(solution)/shard_map/reduce_sum | solution.py:36
  3.3 0.5 collective-permute-start.1
  3.8 0.0 collective-permute-start
  3.8 0.5 collective-permute-start.3
  4.3 0.0 collective-permute-start.2
  4.3 35.8 %all-reduce = (f32[]{:T(128)}, f32[]{:T(128)}, f32[]{:T(128)}, f32[]{:T(128)}) all-reduce(f32[]{:T(128)} %get-tuple-element.8, f32[]{:T(128)} %get-tuple-element.7, f32[]{:T(128)} %get-tuple-element.6, f32[]{:T(128)} %get-tuple-element.5), channel_id=1, replica_groups=mesh['shard'=16,'task'=2] {'shard'}, use_global_device_ids=true, to_apply=%region_18.19 | all-reduce | flops 4 | bytes 32 | tf_op jit(solution)/shard_map/psum | solution.py:36
  42.6 0.0 copy-done.1
  42.6 0.7 fusion.23
  43.3 0.0 collective-permute-done.1
  43.4 0.0 collective-permute-done
  43.4 0.0 collective-permute-done.3
  43.5 0.0 collective-permute-done.2
  43.5 0.0 copy-done
  43.6 6.6 %fusion.8 = (f32[16,16384]{1,0:T(8,128)S(1)}, f32[16,16384]{1,0:T(8,128)}, f32[16,16384]{1,0:T(8,128)}, f32[16,16384]{1,0:T(8,128)}) fusion(s32[1,4,16,16384]{3,2,1,0:T(8,128)} %param.4, f32[16384]{0:T(1024)S(1)} %convert_element_type.63, s32[]{:T(128)} %get-tuple-element.13, bf16[1,4,16,16384]{3,2,1,0:T(8,128)(2,1)S(1)} %copy-done, ...), kind=kLoop, calls=%fused_computation.16 | loop fusion | flops 4194304 | bytes 10747920 | tf_op jit(solution)/shard_map/jit(_where)/select_n | solution.py:40
  50.2 95.0 %all-reduce.3 = (bf16[16,16384]{1,0:T(8,128)(2,1)S(1)}, bf16[16,16384]{1,0:T(8,128)(2,1)S(1)}, bf16[16,16384]{1,0:T(8,128)(2,1)S(1)}, bf16[16,16384]{1,0:T(8,128)(2,1)S(1)}) all-reduce(f32[16,16384]{1,0:T(8,128)} %get-tuple-element.27, f32[16,16384]{1,0:T(8,128)} %get-tuple-element.28, ...), channel_id=1, replica_groups=mesh['shard'=16,'task'=2] {'task'}, use_global_device_ids=true, to_apply=%region_19.20 | all-reduce | flops 1048576 | bytes 6291456 | tf_op jit(solution)/shard_map/psum | solution.py:43
  145.3 1.1 pad_maximum_fusion
  (10 shorter events, 0.2 us)
Async XLA Ops:
  0.0 43.6 %copy-start = (bf16[1,4,16,16384]{3,2,1,0:T(8,128)(2,1)S(1)}, bf16[1,4,16,16384]{3,2,1,0:T(8,128)(2,1)}, u32[]{:S(2)}) copy-start(bf16[1,4,16,16384]{3,2,1,0:T(8,128)(2,1)} %param.3) | copy-start | bytes 6291460
  0.0 42.6 %copy-start.1 = (s32[1,4,8]{2,1,0:T(4,128)S(1)}, s32[1,4,8]{2,1,0:T(4,128)}, u32[]{:S(2)}) copy-start(s32[1,4,8]{2,1,0:T(4,128)} %param.5) | copy-start | bytes 388
  3.3 40.0 %collective-permute-start.1 = (f32[16384]{0:T(1024)S(1)}, f32[16384]{0:T(1024)S(1)}, u32[]{:S(2)}, u32[]{:S(2)}) collective-permute-start(f32[16384]{0:T(1024)S(1)} %get-tuple-element.9), channel_id=1, source_target_pairs={{0,2},{2,0},{4,6},{6,4},{8,10},{10,8},{12,14},{14,12},{16,18},{18,... | collective-permute-start | bytes 196616 | tf_op jit(solution)/shard_map/ppermute | solution.py:13
  3.8 39.5 %collective-permute-start = (f32[16384]{0:T(1024)S(1)}, f32[16384]{0:T(1024)S(1)}, u32[]{:S(2)}, u32[]{:S(2)}) collective-permute-start(f32[16384]{0:T(1024)S(1)} %get-tuple-element.10), channel_id=1, source_target_pairs={{0,2},{2,0},{4,6},{6,4},{8,10},{10,8},{12,14},{14,12},{16,18},{18,... | collective-permute-start | bytes 196616 | tf_op jit(solution)/shard_map/ppermute | solution.py:13
  3.8 39.6 %collective-permute-start.3 = (f32[16384]{0:T(1024)S(1)}, f32[16384]{0:T(1024)S(1)}, u32[]{:S(2)}, u32[]{:S(2)}) collective-permute-start(f32[16384]{0:T(1024)S(1)} %get-tuple-element.11), channel_id=1, source_target_pairs={{0,2},{2,0},{4,6},{6,4},{8,10},{10,8},{12,14},{14,12},{16,18},{18,... | collective-permute-start | bytes 196616 | tf_op jit(solution)/shard_map/ppermute | solution.py:13
  4.3 39.2 %collective-permute-start.2 = (f32[16384]{0:T(1024)S(1)}, f32[16384]{0:T(1024)S(1)}, u32[]{:S(2)}, u32[]{:S(2)}) collective-permute-start(f32[16384]{0:T(1024)S(1)} %get-tuple-element.12), channel_id=1, source_target_pairs={{0,2},{2,0},{4,6},{6,4},{8,10},{10,8},{12,14},{14,12},{16,18},{18,... | collective-permute-start | bytes 196616 | tf_op jit(solution)/shard_map/ppermute | solution.py:13
where the time goes:
time: 147 us; the launch traced here: 146 us
  blocking collectives  131 us (89%)
  other arithmetic  11.8 us (8%)
  between operations  2.65 us (2%)
    psum x1, blocking collectives, on_device(): summed = lax.psum(retained, 'task')  95 us
    psum x1, blocking collectives, on_device(): grand_sum = lax.psum(jnp.sum(magnitude), 'shard')  35.8 us
    select_n x1, other arithmetic, on_device(): jnp.where(rank_scores[0, layer_at] < own_limit, change / probability[None...  6.62 us
    reduce_sum x1, other arithmetic, on_device(): grand_sum = lax.psum(jnp.sum(magnitude), 'shard')  3.31 us
  transfers between devices with their start and end apart: 4, of which 0 were waited for; matrix products, arithmetic and copies ran while one was open for 1% of the time, Pallas kernels for 0%

commit v1 on v0

v1 whole, which is shorter than its diff:
```python
import functools
import jax
import jax.numpy as jnp
from jax import lax
from jax.experimental import pallas as pl
from jax.experimental.pallas import tpu as pltpu
from jax.sharding import PartitionSpec as P

EXPERTS = 8
F32 = jnp.float32
MESH = pl.DeviceIdType.MESH


def kernel(
    sizes, delta_hbm, score_hbm, limit_ref, out_hbm,
    delta, score, outgoing, incoming, sums, sums_in, part, part_in,
    chance, chance_in, own_rate, in_rate, own_kept, merged,
    load_sem, send_sem, recv_sem, sums_sem, part_sem, chance_sem, out_sem,
):
    layers, rows, width, tasks, shards = sizes
    columns = width // tasks
    piece = min(2048, columns)
    pieces = columns // piece
    groups = shards // EXPERTS
    group_bits = groups.bit_length() - 1
    all_bits = shards.bit_length() - 1
    me_shard, me_task = lax.axis_index("shard"), lax.axis_index("task")
    expert = me_shard // groups
    row_total = rows * groups

    def xor_peer(bit):
        stride = 2**bit
        odd = lax.rem(me_shard // stride, 2)
        return me_shard + stride * (1 - 2 * odd)

    def task_peer(k):
        return lax.rem(me_task + k, tasks)

    barrier = pltpu.get_barrier_semaphore()
    for k in range(1, tasks):
        pl.semaphore_signal(barrier, inc=1, device_id={"task": task_peer(k)}, device_id_type=MESH)
    for bit in range(all_bits):
        pl.semaphore_signal(barrier, inc=1, device_id={"shard": xor_peer(bit)}, device_id_type=MESH)

    loads = {}

    def start_load(l, k):
        at = pl.ds(pl.multiple_of(task_peer(k) * columns, 128), columns)
        loads[l, k] = (
            pltpu.make_async_copy(score_hbm.at[0, l, :, at], score.at[l, k], load_sem.at[l, k, 0]),
            pltpu.make_async_copy(delta_hbm.at[0, l, :, at], delta.at[l, k], load_sem.at[l, k, 1]),
        )
        for copy in loads[l, k]:
            copy.start()

    def wait_load(l, k):
        for copy in loads[l, k]:
            copy.wait()

    for l in range(layers):
        for k in range(1, tasks):
            start_load(l, k)
    for l in range(layers):
        start_load(l, 0)

    def at_piece(i):
        return pl.ds(i * piece if isinstance(i, int) else pl.multiple_of(i * piece, 128), piece)

    def masked(l, k, at):
        limit = limit_ref[0, l, expert]
        return jnp.where(score[l, k, :, at] < limit, delta[l, k, :, at].astype(F32), 0.0)

    sends = {}

    def start_send(l, k, i):
        at = at_piece(i)
        copy = pltpu.make_async_remote_copy(
            src_ref=outgoing.at[l, k - 1, :, at],
            dst_ref=incoming.at[l, k - 1, :, at],
            send_sem=send_sem.at[l, k - 1, i],
            recv_sem=recv_sem.at[l, k - 1, i],
            device_id={"task": task_peer(k)},
            device_id_type=MESH,
        )
        copy.start()
        sends[l, k, i] = copy

    ready = []
    entered = False
    for l in range(layers):
        for k in range(1, tasks):
            wait_load(l, k)
            for i in range(pieces):
                at = at_piece(i)
                outgoing[l, k - 1, :, at] = masked(l, k, at).astype(jnp.bfloat16)
                if not entered and ready:
                    pl.semaphore_wait(barrier, tasks - 1 + all_bits)
                    entered = True
                if ready and ready[0][0] < layers - 1:
                    start_send(*ready.pop(0))
                ready.append((l, k, i))

    for k in range(tasks):
        for l in range(layers):
            if k == 0:
                wait_load(l, 0)

            def add_up(i, carry, k=k, l=l):
                at = at_piece(i)
                size = jnp.abs(delta[l, k, :, at].astype(F32))
                sums[k, l : l + 1, at] = jnp.sum(size, axis=0, keepdims=True)
                return carry

            lax.fori_loop(0, pieces, add_up, 0)

    def hold_own(l):
        def body(i, carry):
            at = at_piece(i)
            own_kept[l, :, at] = masked(l, 0, at)
            return carry

        lax.fori_loop(0, pieces, body, 0)

    hold_own(0)
    for bit in range(group_bits):
        copy = pltpu.make_async_remote_copy(
            src_ref=sums, dst_ref=sums_in.at[bit],
            send_sem=sums_sem.at[bit, 0], recv_sem=sums_sem.at[bit, 1],
            device_id={"shard": xor_peer(bit)}, device_id_type=MESH,
        )
        copy.start()
        copy.wait()
        for k in range(tasks):

            def join(i, carry, k=k, bit=bit):
                at = at_piece(i)
                sums[k, :, at] = sums[k, :, at] + sums_in[bit, k, :, at]
                return carry

            lax.fori_loop(0, pieces, join, 0)

    total = jnp.zeros((layers, 128), F32)
    for k in range(tasks):

        def gather(i, carry, k=k):
            block = sums[k, :, at_piece(i)]
            for j in range(piece // 128):
                carry = carry + block[:, j * 128 : (j + 1) * 128]
            return carry

        total = lax.fori_loop(0, pieces, gather, total)

    for step, bit in enumerate(range(group_bits, all_bits)):
        part[step] = total
        if step + 1 < layers:
            hold_own(step + 1)
        copy = pltpu.make_async_remote_copy(
            src_ref=part.at[step], dst_ref=part_in.at[step],
            send_sem=part_sem.at[step, 0], recv_sem=part_sem.at[step, 1],
            device_id={"shard": xor_peer(bit)}, device_id_type=MESH,
        )
        copy.start()
        copy.wait()
        total = total + part_in[step]
    for l in range(all_bits - group_bits + 1, layers):
        hold_own(l)
    grand_mean = jnp.sum(total, axis=1, keepdims=True) / (EXPERTS * row_total * width)

    for k in list(range(1, tasks)) + [0]:

        def rate(i, carry, k=k):
            at = at_piece(i)
            mean = sums[k, :, at] / row_total
            keep = (0.2 + 0.7 * mean / (mean + grand_mean)).astype(jnp.bfloat16)
            if k:
                chance[k - 1, :, at] = keep
            else:
                own_rate[:, at] = 1.0 / keep.astype(F32)
            return carry

        lax.fori_loop(0, pieces, rate, 0)
    chances = []
    for k in range(1, tasks):
        copy = pltpu.make_async_remote_copy(
            src_ref=chance.at[k - 1], dst_ref=chance_in.at[k - 1],
            send_sem=chance_sem.at[k - 1, 0], recv_sem=chance_sem.at[k - 1, 1],
            device_id={"task": task_peer(k)}, device_id_type=MESH,
        )
        copy.start()
        chances.append(copy)
    while ready:
        start_send(*ready.pop(0))

    for l in range(layers):

        def rescale(i, carry, l=l):
            at = at_piece(i)
            own_kept[l, :, at] = own_kept[l, :, at] * own_rate[l : l + 1, at]
            return carry

        lax.fori_loop(0, pieces, rescale, 0)

    for k in range(1, tasks):
        chances[k - 1].wait()

        def invert(i, carry, k=k):
            at = at_piece(i)
            in_rate[k - 1, :, at] = 1.0 / chance_in[k - 1, :, at].astype(F32)
            return carry

        lax.fori_loop(0, pieces, invert, 0)

    stores = []
    for l in range(layers):
        for i in range(pieces):
            at = at_piece(i)
            value = own_kept[l, :, at]
            for k in range(1, tasks):
                sends[l, k, i].wait()
                value = value + incoming[l, k - 1, :, at].astype(F32) * in_rate[k - 1, l : l + 1, at]
            merged[l, :, at] = value.astype(jnp.bfloat16)
            copy = pltpu.make_async_copy(merged.at[l, :, at], out_hbm.at[l, :, at], out_sem.at[l, i])
            copy.start()
            stores.append(copy)
    for copy in stores:
        copy.wait()


def on_device(task_deltas, rank_scores, keep_limits):
    tasks, shards = lax.axis_size("task"), lax.axis_size("shard")
    _, layers, rows, width = task_deltas.shape
    columns = width // tasks
    pieces = columns // min(2048, columns)
    others = max(tasks - 1, 1)
    groups = shards // EXPERTS
    group_bits = max(groups.bit_length() - 1, 1)
    rest_bits = max(shards.bit_length() - groups.bit_length(), 1)
    half = jnp.bfloat16
    dma = pltpu.SemaphoreType.DMA
    return pl.pallas_call(
        functools.partial(kernel, (layers, rows, width, tasks, shards)),
        out_shape=jax.ShapeDtypeStruct((layers, rows, columns), half),
        in_specs=[
            pl.BlockSpec(memory_space=pl.ANY),
            pl.BlockSpec(memory_space=pl.ANY),
            pl.BlockSpec(memory_space=pltpu.SMEM),
        ],
        out_specs=pl.BlockSpec(memory_space=pl.ANY),
        scratch_shapes=[
            pltpu.VMEM((layers, tasks, rows, columns), half),
            pltpu.VMEM((layers, tasks, rows, columns), jnp.int32),
            pltpu.VMEM((layers, others, rows, columns), half),
            pltpu.VMEM((layers, others, rows, columns), half),
            pltpu.VMEM((tasks, layers, columns), F32),
            pltpu.VMEM((group_bits, tasks, layers, columns), F32),
            pltpu.VMEM((rest_bits, layers, 128), F32),
            pltpu.VMEM((rest_bits, layers, 128), F32),
            pltpu.VMEM((others, layers, columns), half),
            pltpu.VMEM((others, layers, columns), half),
            pltpu.VMEM((layers, columns), F32),
            pltpu.VMEM((others, layers, columns), F32),
            pltpu.VMEM((layers, rows, columns), F32),
            pltpu.VMEM((layers, rows, columns), half),
            dma((layers, tasks, 2)),
            dma((layers, others, pieces)),
            dma((layers, others, pieces)),
            dma((group_bits, 2)),
            dma((rest_bits, 2)),
            dma((others, 2)),
            dma((layers, pieces)),
        ],
        compiler_params=pltpu.CompilerParams(
            collective_id=0, has_side_effects=True, vmem_limit_bytes=60 * 2**20
        ),
        name="merge",
    )(task_deltas, rank_scores, keep_limits)


def solution(mesh):
    return jax.shard_map(
        on_device,
        mesh=mesh,
        in_specs=(
            P("task", None, "shard", None),
            P("task", None, "shard", None),
            P("task", None, None),
        ),
        out_specs=P(None, "shard", "task"),
        check_vma=False,
    )
```

time: 147 us -> 34.4 us (0.23)
  blocking collectives: 131 us -> 0 us
  Pallas kernels: 0 us -> 31.9 us
  other arithmetic: 11.8 us -> 0 us
  between operations: 2.65 us -> 0.01 us
  local copies, waits for them, and re-layouts: 0.1 us -> 2.26 us
    psum x2 -> x0, blocking collectives: 131 us -> none  [the longest x1 95 us: on_device(): summed = lax.psum(retained, 'task')]
    pallas_call x0 -> x1, Pallas kernels: none -> 31.9 us  [on_device(): pl.pallas_call(functools.partial(kernel, (layers, rows, width, tasks, sha...]
    select_n x1 -> x0, other arithmetic: 6.62 us -> none  [on_device(): jnp.where(rank_scores[0, layer_at] < own_limit, change / probability[None...]
    reduce_sum x2 -> x0, other arithmetic: 3.98 us -> none  [the longest x1 3.31 us: on_device(): grand_sum = lax.psum(jnp.sum(magnitude), 'shard')]
    unnamed x4 -> x1, local copies, waits for them, and re-layouts: 0.01 us -> 2.26 us
  transfers between devices with their start and end apart: 4 -> 0, of which waited for: 0 -> 0; matrix products, arithmetic and copies ran while one was open for 1% -> 0% of each run, Pallas kernels for 0% -> 0%
where the time goes in v1:
time: 34.4 us; the launch traced here: 34.2 us
  Pallas kernels  31.9 us (93%)
  local copies, waits for them, and re-layouts  2.26 us (7%)
    pallas_call x1, Pallas kernels, on_device(): pl.pallas_call(functools.partial(kernel, (layers, rows, width, tasks, sha...  31.9 us
    unnamed x1, local copies, waits for them, and re-layouts  2.26 us

profile of v1, /device:TPU:0, one launch (start us, length us, event | category | flops | bytes accessed | tf_op | source)
XLA Modules:
  0.0 34.2 jit_solution(13594346141730772903)
XLA Ops:
  0.0 31.9 %merge.1 = bf16[4,16,8192]{2,1,0:T(8,128)(2,1)} custom-call(bf16[1,4,16,16384]{3,2,1,0:T(8,128)(2,1)} %delta_hbm.1, s32[1,4,16,16384]{3,2,1,0:T(8,128)} %score_hbm.1, s32[1,4,8]{2,1,0:T(4,128)} %limit_ref.1), custom_call_target="tpu_custom_call" | custom-call | tf_op jit(solution)/shard_map/merge/pallas_call | solution.py:240
  31.9 2.3 %copy.5 = bf16[4,16,8192]{2,1,0:T(8,128)(2,1)} copy(bf16[4,16,8192]{2,1,0:T(8,128)(2,1)} %merge.1) | data formatting | bytes 2097152

commit v2 on v1

--- a/solution.py
+++ b/solution.py
@@ -12,14 +12,14 @@
 
 
 def kernel(
-    sizes, delta_hbm, score_hbm, limit_ref, out_hbm,
-    delta, score, outgoing, incoming, sums, sums_in, part, part_in,
-    chance, chance_in, own_rate, in_rate, own_kept, merged,
-    load_sem, send_sem, recv_sem, sums_sem, part_sem, chance_sem, out_sem,
+    sizes, delta_hbm, score_hbm, limit_hbm, merged,
+    limit_ref, delta, score, outgoing, incoming, sums, sums_in, part, part_in,
+    chance, chance_in, own_rate, in_rate, own_kept,
+    limit_sem, load_sem, send_sem, recv_sem, sums_sem, part_sem, chance_sem, share_sem,
 ):
     layers, rows, width, tasks, shards = sizes
     columns = width // tasks
-    piece = min(2048, columns)
+    piece = min(4096, columns)
     pieces = columns // piece
     groups = shards // EXPERTS
     group_bits = groups.bit_length() - 1
@@ -28,46 +28,59 @@
     expert = me_shard // groups
     row_total = rows * groups
 
+    def flipped(index, mask):
+        for bit in range(all_bits):
+            stride = 2**bit
+            if mask & stride:
+                index = index + stride * (1 - 2 * lax.rem(index // stride, 2))
+        return index
+
     def xor_peer(bit):
-        stride = 2**bit
-        odd = lax.rem(me_shard // stride, 2)
-        return me_shard + stride * (1 - 2 * odd)
+        return flipped(me_shard, 2**bit)
 
     def task_peer(k):
         return lax.rem(me_task + k, tasks)
 
+    limit_copy = pltpu.make_async_copy(limit_hbm.at[0], limit_ref, limit_sem)
+    limit_copy.start()
     barrier = pltpu.get_barrier_semaphore()
     for k in range(1, tasks):
         pl.semaphore_signal(barrier, inc=1, device_id={"task": task_peer(k)}, device_id_type=MESH)
-    for bit in range(all_bits):
-        pl.semaphore_signal(barrier, inc=1, device_id={"shard": xor_peer(bit)}, device_id_type=MESH)
+    greeted = list(range(1, groups)) + [2**bit for bit in range(group_bits, all_bits)]
+    for mask in greeted:
+        pl.semaphore_signal(
+            barrier, inc=1, device_id={"shard": flipped(me_shard, mask)}, device_id_type=MESH
+        )
 
     loads = {}
 
     def start_load(l, k):
-        at = pl.ds(pl.multiple_of(task_peer(k) * columns, 128), columns)
-        loads[l, k] = (
-            pltpu.make_async_copy(score_hbm.at[0, l, :, at], score.at[l, k], load_sem.at[l, k, 0]),
-            pltpu.make_async_copy(delta_hbm.at[0, l, :, at], delta.at[l, k], load_sem.at[l, k, 1]),
-        )
-        for copy in loads[l, k]:
-            copy.start()
-
-    def wait_load(l, k):
-        for copy in loads[l, k]:
+        cuts = pieces if l == 0 and k else 1
+        length = columns // cuts
+        for i in range(cuts):
+            here = pl.ds(i * length, length)
+            there = pl.ds(pl.multiple_of(task_peer(k) * columns + i * length, 128), length)
+            loads[l, k, i] = [
+                pltpu.make_async_copy(whole.at[0, l, :, there], held.at[l, k, :, here], load_sem.at[l, k, i, j])
+                for j, (whole, held) in enumerate(((score_hbm, score), (delta_hbm, delta)))
+            ]
+            for copy in loads[l, k, i]:
+                copy.start()
+
+    def wait_load(l, k, i):
+        for copy in loads.get((l, k, i), ()):
             copy.wait()
 
     for l in range(layers):
         for k in range(1, tasks):
             start_load(l, k)
-    for l in range(layers):
-        start_load(l, 0)
+    limit_copy.wait()
 
     def at_piece(i):
         return pl.ds(i * piece if isinstance(i, int) else pl.multiple_of(i * piece, 128), piece)
 
     def masked(l, k, at):
-        limit = limit_ref[0, l, expert]
+        limit = limit_ref[l, expert]
         return jnp.where(score[l, k, :, at] < limit, delta[l, k, :, at].astype(F32), 0.0)
 
     sends = {}
@@ -89,21 +102,26 @@
     entered = False
     for l in range(layers):
         for k in range(1, tasks):
-            wait_load(l, k)
             for i in range(pieces):
+                wait_load(l, k, i)
                 at = at_piece(i)
                 outgoing[l, k - 1, :, at] = masked(l, k, at).astype(jnp.bfloat16)
                 if not entered and ready:
-                    pl.semaphore_wait(barrier, tasks - 1 + all_bits)
+                    pl.semaphore_wait(barrier, tasks - 1 + len(greeted))
                     entered = True
+                    owed = True
                 if ready and ready[0][0] < layers - 1:
                     start_send(*ready.pop(0))
+                    if owed:
+                        owed = False
+                        for own in range(layers):
+                            start_load(own, 0)
                 ready.append((l, k, i))
 
     for k in range(tasks):
         for l in range(layers):
             if k == 0:
-                wait_load(l, 0)
+                wait_load(l, 0, 0)
 
             def add_up(i, carry, k=k, l=l):
                 at = at_piece(i)
@@ -180,9 +198,11 @@
 
         lax.fori_loop(0, pieces, rate, 0)
     chances = []
+    segment = columns // groups
+    mine = pl.ds(pl.multiple_of(lax.rem(me_shard, groups) * segment, 128), segment)
     for k in range(1, tasks):
         copy = pltpu.make_async_remote_copy(
-            src_ref=chance.at[k - 1], dst_ref=chance_in.at[k - 1],
+            src_ref=chance.at[k - 1, :, mine], dst_ref=chance_in.at[k - 1, :, mine],
             send_sem=chance_sem.at[k - 1, 0], recv_sem=chance_sem.at[k - 1, 1],
             device_id={"task": task_peer(k)}, device_id_type=MESH,
         )
@@ -200,8 +220,20 @@
 
         lax.fori_loop(0, pieces, rescale, 0)
 
+    shares = {}
     for k in range(1, tasks):
         chances[k - 1].wait()
+        for mask in range(1, groups):
+            copy = pltpu.make_async_remote_copy(
+                src_ref=chance_in.at[k - 1, :, mine], dst_ref=chance_in.at[k - 1, :, mine],
+                send_sem=share_sem.at[k - 1, mask - 1, 0], recv_sem=share_sem.at[k - 1, mask - 1, 1],
+                device_id={"shard": flipped(me_shard, mask)}, device_id_type=MESH,
+            )
+            copy.start()
+            shares[k, mask] = copy
+    for k in range(1, tasks):
+        for mask in range(1, groups):
+            shares[k, mask].wait()
 
         def invert(i, carry, k=k):
             at = at_piece(i)
@@ -210,7 +242,6 @@
 
         lax.fori_loop(0, pieces, invert, 0)
 
-    stores = []
     for l in range(layers):
         for i in range(pieces):
             at = at_piece(i)
@@ -219,34 +250,37 @@
                 sends[l, k, i].wait()
                 value = value + incoming[l, k - 1, :, at].astype(F32) * in_rate[k - 1, l : l + 1, at]
             merged[l, :, at] = value.astype(jnp.bfloat16)
-            copy = pltpu.make_async_copy(merged.at[l, :, at], out_hbm.at[l, :, at], out_sem.at[l, i])
-            copy.start()
-            stores.append(copy)
-    for copy in stores:
-        copy.wait()
+
+
+def put_out(value, out_hbm, sem):
+    copy = pltpu.make_async_copy(value, out_hbm, sem)
+    copy.start()
+    copy.wait()
 
 
 def on_device(task_deltas, rank_scores, keep_limits):
     tasks, shards = lax.axis_size("task"), lax.axis_size("shard")
     _, layers, rows, width = task_deltas.shape
     columns = width // tasks
-    pieces = columns // min(2048, columns)
+    pieces = columns // min(4096, columns)
     others = max(tasks - 1, 1)
     groups = shards // EXPERTS
     group_bits = max(groups.bit_length() - 1, 1)
     rest_bits = max(shards.bit_length() - groups.bit_length(), 1)
     half = jnp.bfloat16
     dma = pltpu.SemaphoreType.DMA
-    return pl.pallas_call(
+    keep_limits = pltpu.with_memory_space_constraint(keep_limits, pltpu.HBM)
+    result = pl.pallas_call(
         functools.partial(kernel, (layers, rows, width, tasks, shards)),
         out_shape=jax.ShapeDtypeStruct((layers, rows, columns), half),
         in_specs=[
-            pl.BlockSpec(memory_space=pl.ANY),
-            pl.BlockSpec(memory_space=pl.ANY),
-            pl.BlockSpec(memory_space=pltpu.SMEM),
+            pl.BlockSpec(memory_space=pltpu.HBM),
+            pl.BlockSpec(memory_space=pltpu.HBM),
+            pl.BlockSpec(memory_space=pltpu.HBM),
         ],
-        out_specs=pl.BlockSpec(memory_space=pl.ANY),
+        out_specs=pl.BlockSpec(memory_space=pltpu.VMEM),
         scratch_shapes=[
+            pltpu.SMEM(keep_limits.shape[1:], jnp.int32),
             pltpu.VMEM((layers, tasks, rows, columns), half),
             pltpu.VMEM((layers, tasks, rows, columns), jnp.int32),
             pltpu.VMEM((layers, others, rows, columns), half),
@@ -260,20 +294,29 @@
             pltpu.VMEM((layers, columns), F32),
             pltpu.VMEM((others, layers, columns), F32),
             pltpu.VMEM((layers, rows, columns), F32),
-            pltpu.VMEM((layers, rows, columns), half),
-            dma((layers, tasks, 2)),
+            dma(()),
+            dma((layers, tasks, pieces, 2)),
             dma((layers, others, pieces)),
             dma((layers, others, pieces)),
             dma((group_bits, 2)),
             dma((rest_bits, 2)),
             dma((others, 2)),
-            dma((layers, pieces)),
+            dma((others, max(groups - 1, 1), 2)),
         ],
         compiler_params=pltpu.CompilerParams(
-            collective_id=0, has_side_effects=True, vmem_limit_bytes=60 * 2**20
+            collective_id=0, has_side_effects=True, vmem_limit_bytes=52 * 2**20
         ),
         name="merge",
     )(task_deltas, rank_scores, keep_limits)
+    return pl.pallas_call(
+        put_out,
+        out_shape=jax.ShapeDtypeStruct(result.shape, result.dtype),
+        in_specs=[pl.BlockSpec(memory_space=pltpu.VMEM)],
+        out_specs=pl.BlockSpec(memory_space=pltpu.HBM),
+        scratch_shapes=[dma(())],
+        compiler_params=pltpu.CompilerParams(vmem_limit_bytes=4 * 2**20),
+        name="put",
+    )(result)
 
 
 def solution(mesh):

time: 34.4 us -> 30.9 us (0.90)
  local copies, waits for them, and re-layouts: 2.26 us -> 0 us
  Pallas kernels: 31.9 us -> 30.7 us
    unnamed x1 -> x0, local copies, waits for them, and re-layouts: 2.26 us -> none
    pallas_call x1, Pallas kernels: 31.9 us -> 29.7 us  [on_device(): pl.pallas_call(functools.partial(kernel, (layers, rows, width, tasks, sha...]
    pallas_call x0 -> x1, Pallas kernels: none -> 0.98 us  [on_device(): pl.pallas_call(put_out, out_shape=jax.ShapeDtypeStruct(result.shape, resu...]
where the time goes in v2:
time: 30.9 us; the launch traced here: 30.7 us
  Pallas kernels  30.7 us (99%)
    pallas_call x1, Pallas kernels, on_device(): pl.pallas_call(functools.partial(kernel, (layers, rows, width, tasks, sha...  29.7 us
    pallas_call x1, Pallas kernels, on_device(): pl.pallas_call(put_out, out_shape=jax.ShapeDtypeStruct(result.shape, resu...  0.98 us

profile of v2, /device:TPU:0, one launch (start us, length us, event | category | flops | bytes accessed | tf_op | source)
XLA Modules:
  0.0 30.7 jit_solution(13288653833919866466)
XLA Ops:
  0.0 29.7 %merge.1.value = bf16[4,16,8192]{2,1,0:T(8,128)(2,1)S(1)} custom-call(bf16[1,4,16,16384]{3,2,1,0:T(8,128)(2,1)} %delta_hbm.1, s32[1,4,16,16384]{3,2,1,0:T(8,128)} %score_hbm.1, s32[1,4,8]{2,1,0:T(4,128)} %limit_hbm.1), custom_call_target="tpu_custom_call" | custom-call | tf_op jit(solution)/shard_map/merge/pallas_call | solution.py:273
  29.7 1.0 %put.1 = bf16[4,16,8192]{2,1,0:T(8,128)(2,1)} custom-call(bf16[4,16,8192]{2,1,0:T(8,128)(2,1)S(1)} %merge.1.value), custom_call_target="tpu_custom_call" | custom-call | tf_op jit(solution)/shard_map/put/pallas_call | solution.py:311
